TPU v7x, 32 devices: a whole 2x2x4 slice. The times are simulated.
32 devices in a mesh: dp: 8 (over z, x), rep: 4 (over y, core).
Axes of the slice: x: 2, y: 2, z: 4, core: 2. Of those that a mesh axis runs over, the one named last changes fastest.
Arguments:
- tokens: bfloat16 [65536, 1280], P(('dp', 'rep')), may hold values from -6 to 6
- sketch_map: bfloat16 [65536, 128], P(('dp', 'rep')), may hold values from -0.125 to 0.125
- test_matrix: bfloat16 [4, 1024, 128], P('rep'), may hold values from -0.09375 to 0.09375
Outputs:
- basis: float32 [1280, 128], P('dp')
- factor: float32 [128, 128], replicated
All inputs are finite; a program needn't handle non-finite values.
Results may differ from a plain program's by a relative error of at most 0.0051.
Values may be sent and summed in bfloat16 or wider, within the bound.
A program may use at most 64 MiB of HBM per device.

v0:
```python
import jax
import jax.numpy as jnp
from jax import lax
from jax.sharding import PartitionSpec as P

ITERS = 2


def whole_factor(matrix):
    gram = jnp.dot(
        matrix.T, matrix, precision=lax.Precision.HIGHEST, preferred_element_type=jnp.float32
    )
    lower = jnp.linalg.cholesky(gram)
    return (jax.scipy.linalg.solve_triangular(lower, matrix.T, lower=True).T, lower.T)


def body(tokens, sketch_map, test_matrix):
    width = tokens.shape[1]
    strip = width // lax.axis_size("dp")
    total_tokens = tokens.shape[0] * lax.axis_size("dp") * lax.axis_size("rep")
    sketch = lax.dot_general(
        sketch_map, tokens, (((0,), (0,)), ((), ())), preferred_element_type=jnp.float32
    ).astype(jnp.bfloat16)
    merged = lax.all_to_all(sketch, "dp", split_axis=1, concat_axis=0, tiled=True)
    local_start = lax.dot_general(
        merged, test_matrix[0], (((0,), (0,)), ((), ())), preferred_element_type=jnp.float32
    )
    start = lax.psum(local_start, "rep")
    gathered = lax.all_gather(start, "dp", axis=0, tiled=True)
    current, factor = whole_factor(gathered)
    for step in range(ITERS):
        rounded = current.astype(jnp.bfloat16)
        projected = jnp.dot(tokens, rounded, preferred_element_type=jnp.float32).astype(
            jnp.bfloat16
        )
        local_sum = lax.dot_general(
            tokens, projected, (((0,), (0,)), ((), ())), preferred_element_type=jnp.float32
        )
        summed = lax.psum(local_sum, ("dp", "rep"))
        current, factor = whole_factor(summed / total_tokens)
    owned = lax.dynamic_slice_in_dim(current, lax.axis_index("dp") * strip, strip, 0)
    return (owned, factor)


def solution(mesh):
    return jax.shard_map(
        body,
        mesh=mesh,
        in_specs=(P(("dp", "rep"), None), P(("dp", "rep"), None), P("rep", None, None)),
        out_specs=(P("dp", None), P()),
        check_vma=False,
    )
```

profile of v0, /device:TPU:0, one launch (start us, length us, event | category | flops | bytes accessed | tf_op | source)
XLA Modules:
  0.0 453.5 jit_solution(7895339741333896489)
XLA Ops:
  7.2 0.0 copy-start
  7.2 0.0 copy-start.1
  7.2 0.0 all-reduce.4.cloned.1.call-start
  7.2 1.0 copy-done
  8.2 3.4 convolution_convert_fusion.4
  11.6 0.2 copy.9
  11.8 18.0 %all_to_all.19 = bf16[128,8,160]{0,2,1:T(8,128)(2,1)S(1)} all-to-all(bf16[128,8,160]{0,2,1:T(8,128)(2,1)S(1)} %bitcast.66), channel_id=1, replica_groups=mesh['dp'=8,'rep'=4] {'dp'}, dimensions={1} | all-to-all | bytes 655360 | tf_op jit(solution)/shard_map/all_to_all | solution.py:24
  29.8 0.0 copy-done.1
  29.8 0.9 fusion.10
  30.7 0.0 all-reduce.4.cloned.1.call-update
  30.7 0.0 all-reduce.6.cloned.1.call-start
  30.7 28.8 %all-reduce.4.cloned.1.call-done = f32[160,128]{1,0:T(8,128)} async-done(((f32[160,128]{1,0:T(8,128)}), f32[160,128]{1,0:T(8,128)}) %all-reduce.4.cloned.1.call-update) | async-done | bytes 81936 | tf_op jit(solution)/shard_map/psum | solution.py:28
  59.5 32.0 %all_gather.3 = f32[1280,128]{1,0:T(8,128)S(1)} all-gather(f32[160,128]{1,0:T(8,128)} %all-reduce.4.cloned.1.call-done), channel_id=1, replica_groups=mesh['dp'=8,'rep'=4] {'dp'}, dimensions={0}, use_global_device_ids=true | all-gather | bytes 737280 | tf_op jit(solution)/shard_map/all_gather | solution.py:29
  91.5 1.2 fusion.36
  92.7 0.1 copy.11
  92.8 11.7 %cholesky.59 = f32[128,128]{1,0:T(8,128)S(1)} custom-call(f32[128,128]{1,0:T(8,128)S(1)} %fusion.25), custom_call_target="Cholesky" | custom-call | tf_op jit(solution)/shard_map/jit(cholesky)/cholesky | solution.py:13
  104.6 0.6 compare_reduce_fusion.2
  105.2 0.7 fusion.18
  105.9 9.8 %custom-call.7 = f32[1,128,128]{1,2,0:T(8,128)S(1)} custom-call(f32[1,128,128]{2,1,0:T(8,128)S(1)} %fusion.18), custom_call_target="InvertDiagBlocksLowerTriangular" | custom-call | tf_op jit(solution)/shard_map/jit(_solve_triangular)/triangular_solve | solution.py:14
  115.7 0.8 convolution_convert_fusion.3
  116.5 7.5 %convolution_bitcast_fusion.1 = f32[1280,128]{0,1:T(8,128)} fusion(bf16[2048,1280]{1,0:T(8,128)(2,1)} %param.6, bf16[128,1280]{1,0:T(8,128)(2,1)S(1)} %convolution_convert_fusion.3), kind=kOutput, calls=%fused_computation.1 | convolution fusion | flops 1342439424 | bytes 6225920 | tf_op jit(solution)/shard_map/dot_general | solution.py:36
  124.0 0.0 all-reduce.6.cloned.1.call-update
  124.0 0.2 all-reduce.8.cloned.1.call-start
  124.2 130.7 %all-reduce.6.cloned.1.call-done = f32[1280,128]{0,1:T(8,128)} async-done(((f32[1280,128]{0,1:T(8,128)}), f32[1280,128]{0,1:T(8,128)}) %all-reduce.6.cloned.1.call-update) | async-done | bytes 655376 | tf_op jit(solution)/shard_map/psum | solution.py:39
  255.0 2.0 fusion.8
  257.0 0.1 copy.12
  257.1 11.7 %cholesky.70 = f32[128,128]{1,0:T(8,128)S(1)} custom-call(f32[128,128]{1,0:T(8,128)S(1)} %fusion.23), custom_call_target="Cholesky" | custom-call | tf_op jit(solution)/shard_map/jit(cholesky)/cholesky | solution.py:13
  268.9 0.6 compare_reduce_fusion.1
  269.5 0.7 fusion.19
  270.2 9.8 %custom-call.8 = f32[1,128,128]{1,2,0:T(8,128)S(1)} custom-call(f32[1,128,128]{2,1,0:T(8,128)S(1)} %fusion.19), custom_call_target="InvertDiagBlocksLowerTriangular" | custom-call | tf_op jit(solution)/shard_map/jit(_solve_triangular)/triangular_solve | solution.py:14
  280.0 1.8 convolution_convert_fusion.1
  281.8 7.5 %convolution_bitcast_fusion = f32[1280,128]{0,1:T(8,128)} fusion(bf16[2048,1280]{1,0:T(8,128)(2,1)} %param.6, bf16[128,1280]{1,0:T(8,128)(2,1)S(1)} %convolution_convert_fusion.1), kind=kOutput, calls=%fused_computation | convolution fusion | flops 1342439424 | bytes 6225920 | tf_op jit(solution)/shard_map/dot_general | solution.py:36
  289.3 0.0 all-reduce.8.cloned.1.call-update
  289.3 128.8 %all-reduce.8.cloned.1.call-done = f32[1280,128]{0,1:T(8,128)} async-done(((f32[1280,128]{0,1:T(8,128)}), f32[1280,128]{0,1:T(8,128)}) %all-reduce.8.cloned.1.call-update) | async-done | bytes 655376 | tf_op jit(solution)/shard_map/psum | solution.py:39
  418.1 2.0 fusion.5
  420.1 0.1 copy.13
  420.2 11.9 %cholesky.81 = f32[128,128]{1,0:T(8,128)S(1)} custom-call(f32[128,128]{1,0:T(8,128)S(1)} %fusion.21), custom_call_target="Cholesky" | custom-call | tf_op jit(solution)/shard_map/jit(cholesky)/cholesky | solution.py:13
  432.2 0.6 compare_reduce_fusion
  432.8 0.7 fusion.31
  433.5 9.8 %custom-call.9 = f32[1,128,128]{1,2,0:T(8,128)S(1)} custom-call(f32[1,128,128]{2,1,0:T(8,128)S(1)} %get-tuple-element.9), custom_call_target="InvertDiagBlocksLowerTriangular" | custom-call | tf_op jit(solution)/shard_map/jit(_solve_triangular)/triangular_solve | solution.py:14
  443.3 0.7 copy.14
  444.0 2.3 fusion
  446.3 0.6 dynamic-slice_bitcast_fusion
  (6 shorter events, 0.1 us)
Async XLA Ops:
  7.2 1.0 copy-start
  7.2 22.6 %copy-start.1 = (bf16[1,1024,128]{2,1,0:T(8,128)(2,1)S(1)}, bf16[1,1024,128]{2,1,0:T(8,128)(2,1)}, u32[]{:S(2)}) copy-start(bf16[1,1024,128]{2,1,0:T(8,128)(2,1)} %param.8) | copy-start | bytes 786436
  7.2 52.3 %all-reduce.4.cloned.1.call-start = ((), (), s32[]{:S(2)}) async-start(), calls=%async_computation.1 | async-start | bytes 163840 | tf_op jit(solution)/shard_map/psum | solution.py:28
  30.7 224.3 %all-reduce.6.cloned.1.call-start = ((), (), s32[]{:S(2)}) async-start(), calls=%async_computation.2 | async-start | bytes 1310720 | tf_op jit(solution)/shard_map/psum | solution.py:39
  124.0 294.1 %all-reduce.8.cloned.1.call-start = ((), (), s32[]{:S(2)}) async-start(), calls=%async_computation.3 | async-start | bytes 1310720 | tf_op jit(solution)/shard_map/psum | solution.py:39
Sparse Core Ops, SparseCore 0:
  30.8 28.6 all-reduce.3
  124.1 130.8 all-reduce.5
  289.5 128.6 all-reduce.7
where the time goes:
time: 454 us
  waiting for transfers between devices  288 us (63%)
  other arithmetic  68.8 us (15%)
  blocking collectives  50 us (11%)
  matrix products  29.3 us (6%)
  between operations  13.9 us (3%)
    psum x2, waiting for transfers between devices, body(): summed = lax.psum(local_sum, ('dp', 'rep'))  260 us
    another operation x9, other arithmetic, whole_factor(): lower = jnp.linalg.cholesky(gram)  37.4 us
    all_gather x1, blocking collectives, body(): gathered = lax.all_gather(start, 'dp', axis=0, tiled=True)  32 us
    another operation x5, other arithmetic, whole_factor(): jax.scipy.linalg.solve_triangular(lower, matrix.T, lower=True)  30.7 us
    psum x1, waiting for transfers between devices, body(): start = lax.psum(local_start, 'rep')  28.8 us
    all_to_all x1, blocking collectives, body(): lax.all_to_all(sketch, 'dp', split_axis=1, concat_axis=0, tiled=True)  18 us
    dot_general x2, matrix products, body(): lax.dot_general(tokens, projected, (((0,), (0,)), ((), ())), preferred_el...  15 us
  transfers between devices with their start and end apart: 3, of which 3 were waited for; matrix products, arithmetic and copies ran while one was open for 0% of the time, Pallas kernels for 0%

commit v1 on v0

v1 whole, which is shorter than its diff:
```python
import functools

import jax
import jax.numpy as jnp
from jax import lax
from jax.experimental import pallas as pl
from jax.experimental.pallas import tpu as pltpu
from jax.sharding import PartitionSpec as P

ITERS = 2
BLOCK = 16
SLABS = 4
LOGICAL = pl.DeviceIdType.LOGICAL
FIRST = (((0,), (0,)), ((), ()))
LAST = (((1,), (1,)), ((), ()))
EXACT = lax.Precision.HIGHEST


def when(full, condition, action):
    if full:
        action()
    else:
        pl.when(condition)(action)


def reduce_stage(n, b, g, scale, fill, greeted, z, send, pair, recv, p, ps, pr, s1, r1, s2, r2, s3, r3):
    m = n // 2
    owners, chunk, _ = send.shape
    full = owners == m
    half = owners * chunk
    me = 2 * g + b
    partner = me + 1 - 2 * b
    mine = pl.multiple_of(b * half, 8)
    theirs = pl.multiple_of((1 - b) * half, 8)

    def peer_of(k):
        peer = g + k
        return peer - jnp.where(peer >= m, m, 0)

    def source_of(k):
        peer = g - k
        return peer + jnp.where(peer < 0, m, 0)

    def rows(side, index):
        return pl.ds(pl.multiple_of(side + index * chunk, 8), chunk)

    swap = pltpu.make_async_remote_copy(
        src_ref=z.at[pl.ds(theirs, half)], dst_ref=pair, send_sem=ps, recv_sem=pr,
        device_id=partner, device_id_type=LOGICAL,
    )
    fill(theirs)
    greeted()
    swap.start()
    fill(mine)

    def scatter_copy(k, slot):
        return pltpu.make_async_remote_copy(
            src_ref=send.at[slot], dst_ref=recv.at[k], send_sem=s1.at[k], recv_sem=r1.at[k],
            device_id=2 * peer_of(k) + b, device_id_type=LOGICAL,
        )

    def gather_copy(k):
        return pltpu.make_async_remote_copy(
            src_ref=p.at[rows(mine, g)], dst_ref=p.at[rows(mine, g)], send_sem=s2.at[k], recv_sem=r2.at[k],
            device_id=2 * peer_of(k) + b, device_id_type=LOGICAL,
        )

    def forward_copy(k, index):
        return pltpu.make_async_remote_copy(
            src_ref=p.at[rows(mine, index)], dst_ref=p.at[rows(mine, index)], send_sem=s3.at[k], recv_sem=r3.at[k],
            device_id=partner, device_id_type=LOGICAL,
        )

    swap.wait_recv()

    def scatter(k, carry):
        peer = peer_of(k)

        def go():
            value = z[rows(mine, peer), :] + pair[pl.ds(pl.multiple_of(peer * chunk, 8), chunk), :]
            send[peer] = value.astype(jnp.bfloat16)
            scatter_copy(k, peer).start()

        when(full, peer < owners, go)
        return carry

    lax.fori_loop(1, m, scatter, 0)

    def own():
        total = z[rows(mine, g), :] + pair[pl.ds(pl.multiple_of(g * chunk, 8), chunk), :]

        def add(k, total):
            scatter_copy(k, 0).wait_recv()
            return total + recv[k].astype(jnp.float32)

        total = lax.fori_loop(1, m, add, total)
        p[rows(mine, g), :] = total * scale

        def gather(k, carry):
            gather_copy(k).start()
            return carry

        lax.fori_loop(1, m, gather, 0)
        forward_copy(0, g).start()

    when(full, g < owners, own)

    def collect(k, carry):
        source = source_of(k)

        def go():
            gather_copy(k).wait_recv()
            forward_copy(k, source).start()

        when(full, source < owners, go)
        return carry

    lax.fori_loop(1, m, collect, 0)

    def arrive(k, carry):
        when(full, source_of(k) < owners, lambda: forward_copy(k, 0).wait_recv())
        return carry

    lax.fori_loop(0, m, arrive, 0)

    def finish():
        swap.wait_send()

        def done(k, carry):
            when(full, peer_of(k) < owners, lambda: scatter_copy(k, 0).wait_send())
            when(full, g < owners, lambda: gather_copy(k).wait_send())
            when(full, source_of(k) < owners, lambda: forward_copy(k, 0).wait_send())
            return carry

        lax.fori_loop(1, m, done, 0)
        when(full, g < owners, lambda: forward_copy(0, 0).wait_send())

    return finish


def factorize(p, left, right):
    k = left.shape[0]
    value = p[...]
    left[...] = lax.dot_general(value, value, FIRST, precision=EXACT, preferred_element_type=jnp.float32)
    row = lax.broadcasted_iota(jnp.int32, (k, k), 0)
    col = lax.broadcasted_iota(jnp.int32, (k, k), 1)
    right[...] = jnp.where(row == col, 1.0, 0.0)
    rid = lax.broadcasted_iota(jnp.int32, (BLOCK, k), 0)
    for o in range(0, k, BLOCK):
        a = left[o : o + BLOCK, :]
        e = right[o : o + BLOCK, :]
        cols = [jnp.broadcast_to(a[:, o + t : o + t + 1], (BLOCK, k)) for t in range(BLOCK)]
        for s in range(BLOCK):
            inv = lax.rsqrt(cols[s][s : s + 1, :])
            f = jnp.where(rid > s, cols[s] * inv, 0.0)
            arow = a[s : s + 1, :] * inv
            erow = e[s : s + 1, :] * inv
            a = jnp.where(rid == s, arow, a - f * arow)
            e = jnp.where(rid == s, erow, e - f * erow)
            for t in range(s + 1, BLOCK):
                cols[t] = cols[t] - f * (cols[t][s : s + 1, :] * inv)
        left[o : o + BLOCK, :] = a
        right[o : o + BLOCK, :] = e
        if o + BLOCK < k:
            ua = lax.dot_general(a, a, FIRST, precision=EXACT, preferred_element_type=jnp.float32)
            ue = lax.dot_general(a, e, FIRST, precision=EXACT, preferred_element_type=jnp.float32)
            left[o + BLOCK :, :] = left[o + BLOCK :, :] - ua[o + BLOCK :, :]
            right[o + BLOCK :, :] = right[o + BLOCK :, :] - ue[o + BLOCK :, :]
    return row <= col


def kernel(
    n_dp, n_rep, tokens, smap, test, basis, factor,
    tok, mp, tst, zt, yt, z, vb, send, pair, recv, p, left, right,
    in_sem, ps, pr, s1, r1, s2, r2, s3, r3,
):
    n = n_dp * n_rep
    m = n // 2
    dp = lax.axis_index("dp")
    rep = lax.axis_index("rep")
    b = lax.rem(rep, 2)
    g = lax.div(dp * n_rep + rep - b, 2)
    count, width = tok.shape
    k = mp.shape[1]
    slab = count // SLABS
    strip = width // n_dp

    test_copy = pltpu.make_async_copy(test.at[0, pl.ds(pl.multiple_of(dp * k, k), k)], tst, in_sem.at[2 * SLABS])
    loads = []
    for i in range(SLABS):
        part = pl.ds(i * slab, slab)
        loads.append(pltpu.make_async_copy(tokens.at[part], tok.at[part], in_sem.at[2 * i]))
        loads.append(pltpu.make_async_copy(smap.at[part], mp.at[part], in_sem.at[2 * i + 1]))
    for copy in loads:
        copy.start()
    test_copy.start()

    barrier = pltpu.get_barrier_semaphore()
    pl.semaphore_signal(barrier, inc=1, device_id=2 * g + 1 - b, device_id_type=LOGICAL)

    def greet(i, carry):
        peer = g + i
        peer = peer - jnp.where(peer >= m, m, 0)
        pl.semaphore_signal(barrier, inc=1, device_id=2 * peer + b, device_id_type=LOGICAL)
        return carry

    lax.fori_loop(1, m, greet, 0)

    for i in range(SLABS):
        loads[2 * i].wait()
        loads[2 * i + 1].wait()
        part = slice(i * slab, (i + 1) * slab)
        term = lax.dot_general(mp[part, :], tok[part, :], FIRST, preferred_element_type=jnp.float32)
        zt[...] = term if i == 0 else zt[...] + term
    test_copy.wait()
    span = width // 2

    def fill_start(side):
        part = zt[:, pl.ds(pl.multiple_of(side, k), span)].astype(jnp.bfloat16)
        z[pl.ds(side, span), :] = lax.dot_general(part, tst[...], FIRST, preferred_element_type=jnp.float32)

    def fill_power(side):
        part = tok[:, pl.ds(pl.multiple_of(side, k), span)]
        product = jnp.dot(yt[...], part, preferred_element_type=jnp.float32)
        for j in range(0, span, k):
            z[pl.ds(pl.multiple_of(side + j, 8), k), :] = product[:, j : j + k].T

    for stage in range(ITERS + 1):
        if stage > 0:
            for i in range(SLABS):
                part = slice(i * slab, (i + 1) * slab)
                y = jnp.dot(tok[part, :], vb[...], preferred_element_type=jnp.float32)
                yt[:, part] = y.T.astype(jnp.bfloat16)
        scale = 1.0 if stage == 0 else 1.0 / (count * n)
        finish = reduce_stage(
            n, b, g, scale, fill_power if stage else fill_start,
            (lambda: None) if stage else (lambda: pl.semaphore_wait(barrier, m)), z, send, pair.at[stage], recv.at[stage], p.at[stage],
            ps.at[stage], pr.at[stage], s1.at[stage], r1.at[stage], s2.at[stage], r2.at[stage],
            s3.at[stage], r3.at[stage],
        )
        upper = factorize(p.at[stage], left, right)
        if stage < ITERS:
            vb[...] = lax.dot_general(
                p[stage], right[...], LAST, precision=EXACT, preferred_element_type=jnp.float32
            ).astype(jnp.bfloat16)
        else:
            factor[...] = jnp.where(upper, left[...], 0.0)
            first = dp * strip
            if strip % 8 == 0:
                own = p[stage, pl.ds(pl.multiple_of(first, 8), strip), :]
            else:
                own = p[stage, pl.ds(first, strip), :]
            basis[...] = lax.dot_general(own, right[...], LAST, precision=EXACT, preferred_element_type=jnp.float32)
        finish()


def body(n_dp, n_rep, tokens, smap, test):
    n = n_dp * n_rep
    m = n // 2
    count, width = tokens.shape
    k = smap.shape[1]
    half = width // 2
    chunk = -(-half // (m * 8)) * 8
    owners = half // chunk
    stages = ITERS + 1
    dma = pltpu.SemaphoreType.DMA
    anywhere = pl.BlockSpec(memory_space=pl.ANY)
    vmem = pl.BlockSpec(memory_space=pltpu.VMEM)
    return pl.pallas_call(
        functools.partial(kernel, n_dp, n_rep),
        out_shape=(
            jax.ShapeDtypeStruct((width // n_dp, k), jnp.float32),
            jax.ShapeDtypeStruct((k, k), jnp.float32),
        ),
        in_specs=[anywhere] * 3,
        out_specs=(vmem, vmem),
        scratch_shapes=[
            pltpu.VMEM((count, width), jnp.bfloat16),
            pltpu.VMEM((count, k), jnp.bfloat16),
            pltpu.VMEM((k, k), jnp.bfloat16),
            pltpu.VMEM((k, width), jnp.float32),
            pltpu.VMEM((k, count), jnp.bfloat16),
            pltpu.VMEM((width, k), jnp.float32),
            pltpu.VMEM((width, k), jnp.bfloat16),
            pltpu.VMEM((owners, chunk, k), jnp.bfloat16),
            pltpu.VMEM((stages, half, k), jnp.float32),
            pltpu.VMEM((stages, m, chunk, k), jnp.bfloat16),
            pltpu.VMEM((stages, width, k), jnp.float32),
            pltpu.VMEM((k, k), jnp.float32),
            pltpu.VMEM((k, k), jnp.float32),
            dma((2 * SLABS + 1,)),
            dma((stages,)),
            dma((stages,)),
            dma((stages, m)),
            dma((stages, m)),
            dma((stages, m)),
            dma((stages, m)),
            dma((stages, m)),
            dma((stages, m)),
        ],
        compiler_params=pltpu.CompilerParams(collective_id=0, has_side_effects=True),
    )(tokens, smap, test)


def solution(mesh):
    return jax.shard_map(
        functools.partial(body, mesh.shape["dp"], mesh.shape["rep"]),
        mesh=mesh,
        in_specs=(P(("dp", "rep"), None), P(("dp", "rep"), None), P("rep", None, None)),
        out_specs=(P("dp", None), P()),
        check_vma=False,
    )
```

time: 454 us -> 85.7 us (0.19)
  waiting for transfers between devices: 288 us -> 0 us
  Pallas kernels: 0 us -> 81 us
  other arithmetic: 68.8 us -> 0 us
  blocking collectives: 50 us -> 0 us
  matrix products: 29.3 us -> 0 us
  between operations: 13.9 us -> 0.64 us
    psum x3 -> x0, waiting for transfers between devices: 288 us -> none  [the longest x2 260 us: body(): summed = lax.psum(local_sum, ('dp', 'rep'))]
    pallas_call x0 -> x1, Pallas kernels: none -> 81 us  [body(): pl.pallas_call(functools.partial(kernel, n_dp, n_rep), out_shape=(jax.Sha...]
    another operation x14 -> x0, other arithmetic: 68.1 us -> none  [the longest x9 37.4 us: whole_factor(): lower = jnp.linalg.cholesky(gram)]
    all_gather x1 -> x0, blocking collectives: 32 us -> none  [body(): gathered = lax.all_gather(start, 'dp', axis=0, tiled=True)]
    dot_general x7 -> x0, matrix products: 24.5 us -> none  [the longest x2 15 us: body(): lax.dot_general(tokens, projected, (((0,), (0,)), ((), ())), preferred_el...]
    all_to_all x1 -> x0, blocking collectives: 18 us -> none  [body(): lax.all_to_all(sketch, 'dp', split_axis=1, concat_axis=0, tiled=True)]
    another operation x3 -> x0, matrix products: 4.85 us -> none  [whole_factor(): jax.scipy.linalg.solve_triangular(lower, matrix.T, lower=True)]
  transfers between devices with their start and end apart: 3 -> 0, of which waited for: 3 -> 0; matrix products, arithmetic and copies ran while one was open for 0% -> 0% of each run, Pallas kernels for 0% -> 0%
where the time goes in v1:
time: 85.7 us; the launch traced here: 84.7 us
  Pallas kernels  81 us (95%)
  local copies, waits for them, and re-layouts  3 us (4%)
    pallas_call x1, Pallas kernels, body(): pl.pallas_call(functools.partial(kernel, n_dp, n_rep), out_shape=(jax.Sha...  81 us
    unnamed x2, local copies, waits for them, and re-layouts  3 us

profile of v1, /device:TPU:0, one launch (start us, length us, event | category | flops | bytes accessed | tf_op | source)
XLA Modules:
  0.0 84.7 jit_solution(3648382570747589990)
XLA Ops:
  0.6 81.0 %shard_map.50 = (f32[160,128]{1,0:T(8,128)}, f32[128,128]{1,0:T(8,128)}) custom-call(bf16[2048,1280]{1,0:T(8,128)(2,1)} %tokens.1, bf16[2048,128]{1,0:T(8,128)(2,1)} %smap.1, bf16[1,1024,128]{2,1,0:T(8,128)(2,1)} %test.1), custom_call_target="tpu_custom_call" | custom-call | tf_op jit(solution)/shard_map/pallas_call | solution.py:269
  81.7 1.5 %copy.7 = f32[160,128]{1,0:T(8,128)} copy(f32[160,128]{1,0:T(8,128)} %get-tuple-element.4) | data formatting | bytes 163840
  83.2 1.5 %copy.8 = f32[128,128]{1,0:T(8,128)} copy(f32[128,128]{1,0:T(8,128)} %get-tuple-element.5) | data formatting | bytes 131072
